TPU v7x, 32 devices: a whole 2x2x4 slice. The times are simulated.
32 devices in a mesh: mod: 4 (over y, x), seq: 8 (over z, core).
Axes of the slice: x: 2, y: 2, z: 4, core: 2. Of those that a mesh axis runs over, the one named last changes fastest.
Arguments:
- tokens: bfloat16 [2048, 4096], P(('mod', 'seq')), may hold values from -6 to 6
- norm_gain: float32 [3, 4096], replicated, may hold values from 0.2 to 2.6
- qkv_weight: bfloat16 [3, 4096, 12288], P(None, None, 'seq'), may hold values from -0.45 to 0.45
- out_weight: bfloat16 [3, 4096, 4096], P(None, 'seq'), may hold values from -0.375 to 0.375
- modality: int32 [16], replicated, may hold values from 0 to 2
- doc_lengths: int32 [4], replicated, may hold values from 1 to 1024, 2048 in all
Outputs:
- mixed: bfloat16 [2048, 4096], P(('mod', 'seq'))
Inputs may be any that keep to these rules, and one draw needn't show every extreme that they name: `doc_lengths`: the lengths sum to 2048; documents follow one another from position 0 in the given order.
All inputs are finite; a program needn't handle non-finite values.
Results may differ from a plain program's by a relative error of at most 0.015.
Values may be sent and summed in bfloat16 or wider, within the bound.
A program may use at most 128 MiB of HBM per device.

v0:
```python
import math
import jax
import jax.numpy as jnp
from jax import lax
from jax.sharding import PartitionSpec as P

HDIM = 128
BLOCK = 128


def modes_of_rows(first_row, row_count, modality):
    block_ids = (first_row + jnp.arange(row_count, dtype=jnp.int32)) // BLOCK
    block_table = jnp.arange(modality.shape[0], dtype=jnp.int32)
    picked = jnp.where(block_ids[:, None] == block_table[None, :], modality[None, :], 0)
    return jnp.sum(picked, axis=1)


def documents(positions, doc_lengths):
    doc_ends = jnp.cumsum(doc_lengths)
    return jnp.sum((positions[:, None] >= doc_ends[None, :]).astype(jnp.int32), axis=1)


def body(tokens, norm_gain, qkv_weight, out_weight, modality, doc_lengths):
    row_count = tokens.shape[0]
    seq_count = lax.axis_size("seq")
    mod_count = lax.axis_size("mod")
    group_rows = row_count * seq_count
    mod_index = lax.axis_index("mod")
    own_first = (mod_index * seq_count + lax.axis_index("seq")) * row_count
    row_modes = modes_of_rows(own_first, row_count, modality)
    choose = (
        row_modes[:, None, None] == jnp.arange(norm_gain.shape[0], dtype=jnp.int32)[None, :, None]
    )
    gain_rows = jnp.sum(jnp.where(choose, norm_gain[None, :, :], 0.0), axis=1)
    values = tokens.astype(jnp.float32)
    mean_square = jnp.mean(values * values, axis=1, keepdims=True)
    normed = (values * lax.rsqrt(mean_square + 1e-05) * gain_rows).astype(jnp.bfloat16)
    gathered = lax.all_gather(normed, "seq", axis=0, tiled=True)
    group_first = mod_index * group_rows
    block_count = group_rows // BLOCK
    block_modes = lax.dynamic_slice_in_dim(modality, group_first // BLOCK, block_count)
    heads_here = qkv_weight.shape[2] // (3 * HDIM)

    def project(block_pair):
        row_block, block_mode = block_pair
        weight = lax.dynamic_index_in_dim(qkv_weight, block_mode, 0, keepdims=False)
        return jnp.dot(row_block, weight, preferred_element_type=jnp.float32).astype(jnp.bfloat16)

    projected = lax.map(
        project, (gathered.reshape(block_count, BLOCK, gathered.shape[1]), block_modes)
    )
    projected = projected.reshape(group_rows, heads_here, 3, HDIM)
    queries = projected[:, :, 0, :]
    keys_here = projected[:, :, 1, :]
    values_here = projected[:, :, 2, :]
    quarter = group_rows // mod_count
    local_rows = jnp.arange(group_rows, dtype=jnp.int32)
    query_pos = group_first + local_rows
    query_docs = documents(query_pos, doc_lengths)
    block_size = min(512, quarter)
    block_total = group_rows // block_size
    score_scale = 1.0 / math.sqrt(HDIM)
    query_blocks = queries.reshape(block_total, block_size, heads_here, HDIM)
    pos_blocks = query_pos.reshape(block_total, block_size)
    doc_blocks = query_docs.reshape(block_total, block_size)
    start_state = (
        jnp.full((block_total, heads_here, block_size), -1e30, jnp.float32),
        jnp.zeros((block_total, heads_here, block_size), jnp.float32),
        jnp.zeros((block_total, block_size, heads_here, HDIM), jnp.float32),
    )
    key_start = jnp.int32(0)
    piece_keys = lax.all_gather(keys_here, "mod", axis=0, tiled=True)
    piece_values = lax.all_gather(values_here, "mod", axis=0, tiled=True)
    key_count = piece_keys.shape[0]
    key_pos = jnp.arange(key_count, dtype=jnp.int32)
    key_docs = documents(key_pos, doc_lengths)

    def one_block(block_state):
        row_max, totals, summed_rows, query_block, block_pos, block_docs = block_state

        def attend(unused):
            scores = (
                jnp.einsum(
                    "qhc,khc->hqk", query_block, piece_keys, preferred_element_type=jnp.float32
                )
                * score_scale
            )
            allowed = (
                (key_pos[None, :] <= block_pos[:, None])
                & (key_docs[None, :] == block_docs[:, None])
            )[None, :, :]
            new_max = jnp.maximum(row_max, jnp.max(jnp.where(allowed, scores, -1e30), axis=2))
            weights = jnp.where(allowed, jnp.exp(scores - new_max[:, :, None]), 0.0)
            rescale = jnp.exp(row_max - new_max)
            new_totals = totals * rescale + jnp.sum(weights, axis=2)
            added_rows = jnp.einsum(
                "hqk,khc->qhc",
                weights.astype(jnp.bfloat16),
                piece_values,
                preferred_element_type=jnp.float32,
            )
            new_rows = summed_rows * jnp.transpose(rescale)[:, :, None] + added_rows
            return (new_max, new_totals, new_rows)

        def keep_state(unused):
            return (row_max, totals, summed_rows)

        return lax.cond(key_start <= jnp.max(block_pos), attend, keep_state, 0)

    row_max, totals, summed_rows = lax.map(
        one_block,
        (start_state[0], start_state[1], start_state[2], query_blocks, pos_blocks, doc_blocks),
    )
    divisor = jnp.transpose(totals, (0, 2, 1))[:, :, :, None]
    attended = (summed_rows / divisor).astype(jnp.bfloat16).reshape(group_rows, heads_here * HDIM)

    def output(block_pair):
        row_block, block_mode = block_pair
        weight = lax.dynamic_index_in_dim(out_weight, block_mode, 0, keepdims=False)
        return jnp.dot(row_block, weight, preferred_element_type=jnp.float32)

    partial_value = lax.map(
        output, (attended.reshape(block_count, BLOCK, attended.shape[1]), block_modes)
    )
    head_sums = lax.psum_scatter(
        partial_value.reshape(group_rows, partial_value.shape[2]).astype(jnp.bfloat16),
        "seq",
        scatter_dimension=0,
        tiled=True,
    ).astype(jnp.float32)
    return (tokens.astype(jnp.float32) + head_sums).astype(jnp.bfloat16)


def solution(mesh):
    return jax.shard_map(
        body,
        mesh=mesh,
        in_specs=(
            P(("mod", "seq"), None),
            P(),
            P(None, None, "seq"),
            P(None, "seq", None),
            P(),
            P(),
        ),
        out_specs=P(("mod", "seq"), None),
        check_vma=False,
    )
```

profile of v0, /device:TPU:0, one launch (start us, length us, event | category | flops | bytes accessed | tf_op | source)
XLA Modules:
  0.0 286.2 jit_solution(8059738032792153300)
XLA Ops:
  6.6 0.8 select_reduce_fusion.2
  7.4 1.2 fusion.48
  8.6 1.3 select_reduce_fusion.1
  9.9 2.0 fusion.50
  12.2 49.6 %all-gather.6.cloned.1.call-done = bf16[512,4096]{1,0:T(8,128)(2,1)} async-done(((bf16[64,4096]{1,0:T(8,128)(2,1)}), bf16[512,4096]{1,0:T(8,128)(2,1)}) %all-gather.6.cloned.1.call-update) | async-done | bytes 4194320 | tf_op jit(solution)/shard_map/all_gather | solution.py:38
  61.7 37.1 %while.33 = (s32[]{:T(128)}, bf16[4,128,1536]{2,1,0:T(8,128)(2,1)S(1)}, bf16[4,128,4096]{2,1,0:T(8,128)(2,1)}, s32[4]{0:T(128)S(1)}, bf16[3,4096,1536]{2,1,0:T(8,128)(2,1)}, /*index=5*/s32[]{:T(128)}, s32[]{:T(128)}, s32[]{:T(128)}) while((s32[]{:T(128)}, bf16[4,128,1536]{2,1,0:T(8,128)(2,1)S(1)}, bf16[4,128,4096]{2,1,0:T(8,128)(2,1)}, ...), condition=%wide.region_4.5_spmd, body=%wide.region_3.4_spmd.sunk | while | flops 1610809344 | bytes 14025863 | solution.py:49
  61.7 0.6 dynamic_slice.95
  64.3 6.7 %fusion.65 = bf16[4,128,1536]{2,1,0:T(8,128)(2,1)S(1)} fusion(bf16[4,128,1536]{2,1,0:T(8,128)(2,1)S(1)} %get-tuple-element.457, s32[]{:T(128)} %get-tuple-element.456, bf16[3,4096,1536]{2,1,0:T(8,128)(2,1)} %get-tuple-element.468, s32[]{:T(128)S(6)} %select_n.67, bf16[4,128,4096]{2,1,0:T(8,128)(2,1)} %get-tuple-element.466), kind=kOutput, calls=%fused_computation.6.clone.1 | convolution fusion | flops 1610809344 | bytes 14025732 | tf_op jit(solution)/shard_map/while/body/eval_jaxpr/dot_general | solution.py:47
  71.0 0.6 dynamic_slice.95
  73.5 6.7 %fusion.65 = bf16[4,128,1536]{2,1,0:T(8,128)(2,1)S(1)} fusion(bf16[4,128,1536]{2,1,0:T(8,128)(2,1)S(1)} %get-tuple-element.457, s32[]{:T(128)} %get-tuple-element.456, bf16[3,4096,1536]{2,1,0:T(8,128)(2,1)} %get-tuple-element.468, s32[]{:T(128)S(6)} %select_n.67, bf16[4,128,4096]{2,1,0:T(8,128)(2,1)} %get-tuple-element.466), kind=kOutput, calls=%fused_computation.6.clone.1 | convolution fusion | flops 1610809344 | bytes 14025732 | tf_op jit(solution)/shard_map/while/body/eval_jaxpr/dot_general | solution.py:47
  80.3 0.6 dynamic_slice.95
  82.8 6.7 %fusion.65 = bf16[4,128,1536]{2,1,0:T(8,128)(2,1)S(1)} fusion(bf16[4,128,1536]{2,1,0:T(8,128)(2,1)S(1)} %get-tuple-element.457, s32[]{:T(128)} %get-tuple-element.456, bf16[3,4096,1536]{2,1,0:T(8,128)(2,1)} %get-tuple-element.468, s32[]{:T(128)S(6)} %select_n.67, bf16[4,128,4096]{2,1,0:T(8,128)(2,1)} %get-tuple-element.466), kind=kOutput, calls=%fused_computation.6.clone.1 | convolution fusion | flops 1610809344 | bytes 14025732 | tf_op jit(solution)/shard_map/while/body/eval_jaxpr/dot_general | solution.py:47
  89.5 0.6 dynamic_slice.95
  92.1 6.7 %fusion.65 = bf16[4,128,1536]{2,1,0:T(8,128)(2,1)S(1)} fusion(bf16[4,128,1536]{2,1,0:T(8,128)(2,1)S(1)} %get-tuple-element.457, s32[]{:T(128)} %get-tuple-element.456, bf16[3,4096,1536]{2,1,0:T(8,128)(2,1)} %get-tuple-element.468, s32[]{:T(128)S(6)} %select_n.67, bf16[4,128,4096]{2,1,0:T(8,128)(2,1)} %get-tuple-element.466), kind=kOutput, calls=%fused_computation.6.clone.1 | convolution fusion | flops 1610809344 | bytes 14025732 | tf_op jit(solution)/shard_map/while/body/eval_jaxpr/dot_general | solution.py:47
  98.8 1.1 copy.14
  99.9 0.6 reshape.161
  100.6 1.1 fusion.53
  101.8 0.7 all-gather.10.cloned.1.call-update
  102.9 0.3 copy.15
  103.3 32.5 %all-gather.8.cloned.1.call-done = bf16[2048,4,1,128]{0,3,2,1:T(8,128)(2,1)} async-done(((bf16[512,4,1,128]{0,3,2,1:T(8,128)(2,1)}), bf16[2048,4,1,128]{0,3,2,1:T(8,128)(2,1)}) %all-gather.8.cloned.1.call-update) | async-done | bytes 2097168 | tf_op jit(solution)/shard_map/all_gather | solution.py:72
  135.7 3.0 %copy.17 = bf16[2048,4,128]{2,0,1:T(8,128)(2,1)S(1)} copy(bf16[2048,4,128]{0,2,1:T(8,128)(2,1)} %bitcast.85) | data formatting | bytes 4194304
  138.8 33.9 %all-gather.10.cloned.1.call-done = bf16[2048,4,1,128]{0,3,2,1:T(8,128)(2,1)} async-done(((bf16[512,4,1,128]{0,3,2,1:T(8,128)(2,1)}), bf16[2048,4,1,128]{0,3,2,1:T(8,128)(2,1)}) %all-gather.10.cloned.1.call-update) | async-done | bytes 2097168 | tf_op jit(solution)/shard_map/all_gather | solution.py:73
  172.7 4.0 %copy.18 = bf16[2048,4,128]{2,0,1:T(8,128)(2,1)} copy(bf16[2048,4,128]{0,2,1:T(8,128)(2,1)} %bitcast.86) | data formatting | bytes 4194304
  176.6 23.8 %while.35 = (s32[]{:T(128)}, f32[4,4,128]{2,1,0:T(4,128)S(1)}, f32[4,128,4,128]{1,3,2,0:T(8,128)}, s32[4,128]{1,0:T(4,128)S(1)}, s32[2048]{0:T(1024)S(1)}, /*ind...) while((s32[]{:T(128)}, f32[4,4,128]{2,1,0:T(4,128)S(1)}, ...), condition=%wide.region_14.15_spmd.clone, body=%wide.region_8.14_spmd.clone.sunk | while | flops 549324416 | bytes 28503860 | solution.py:110
  176.6 0.6 fusion.69
  178.0 3.7 %conditional.3 = (f32[1,4,128]{2,1,0:T(4,128)S(1)}, f32[1,128,4,128]{3,1,2,0:T(8,128)S(1)}) conditional(s32[]{:T(128)} %convert_element_type.82, (f32[4,128]{1,0:T(4,128)S(1)}, f32[128,4,128]{2,0,1:T(8,128)S(1)}) %tuple.105, (s32[2048]{0:T(1024)S(1)}, s32[1,128]{1,0:T(1,128)S(1)}, s32[2048]{0:T(1024)S(1)}, s32[4,128]{1,0:T(4,128)S(1)}, s32[]{:T(128)}, ...), branch_computations={%region_10.10_spmd, %region_11.13_spmd} | conditional | flops 549324288 | bytes 26912820 | solution.py:108
  178.0 0.3 compare_and_fusion
  178.3 1.0 select_reduce_fusion
  179.3 1.2 fusion.18
  180.5 1.2 fusion.31
  181.8 0.7 constant_dynamic-update-slice_fusion.5
  182.5 0.6 fusion.69
  183.9 3.7 %conditional.3 = (f32[1,4,128]{2,1,0:T(4,128)S(1)}, f32[1,128,4,128]{3,1,2,0:T(8,128)S(1)}) conditional(s32[]{:T(128)} %convert_element_type.82, (f32[4,128]{1,0:T(4,128)S(1)}, f32[128,4,128]{2,0,1:T(8,128)S(1)}) %tuple.105, (s32[2048]{0:T(1024)S(1)}, s32[1,128]{1,0:T(1,128)S(1)}, s32[2048]{0:T(1024)S(1)}, s32[4,128]{1,0:T(4,128)S(1)}, s32[]{:T(128)}, ...), branch_computations={%region_10.10_spmd, %region_11.13_spmd} | conditional | flops 549324288 | bytes 26912820 | solution.py:108
  183.9 0.3 compare_and_fusion
  184.2 1.0 select_reduce_fusion
  185.2 1.2 fusion.18
  186.4 1.2 fusion.31
  187.7 0.7 constant_dynamic-update-slice_fusion.5
  188.5 0.6 fusion.69
  189.8 3.7 %conditional.3 = (f32[1,4,128]{2,1,0:T(4,128)S(1)}, f32[1,128,4,128]{3,1,2,0:T(8,128)S(1)}) conditional(s32[]{:T(128)} %convert_element_type.82, (f32[4,128]{1,0:T(4,128)S(1)}, f32[128,4,128]{2,0,1:T(8,128)S(1)}) %tuple.105, (s32[2048]{0:T(1024)S(1)}, s32[1,128]{1,0:T(1,128)S(1)}, s32[2048]{0:T(1024)S(1)}, s32[4,128]{1,0:T(4,128)S(1)}, s32[]{:T(128)}, ...), branch_computations={%region_10.10_spmd, %region_11.13_spmd} | conditional | flops 549324288 | bytes 26912820 | solution.py:108
  189.9 0.3 compare_and_fusion
  190.2 1.0 select_reduce_fusion
  191.2 1.2 fusion.18
  192.3 1.2 fusion.31
  193.7 0.7 constant_dynamic-update-slice_fusion.5
  194.4 0.6 fusion.69
  195.8 3.7 %conditional.3 = (f32[1,4,128]{2,1,0:T(4,128)S(1)}, f32[1,128,4,128]{3,1,2,0:T(8,128)S(1)}) conditional(s32[]{:T(128)} %convert_element_type.82, (f32[4,128]{1,0:T(4,128)S(1)}, f32[128,4,128]{2,0,1:T(8,128)S(1)}) %tuple.105, (s32[2048]{0:T(1024)S(1)}, s32[1,128]{1,0:T(1,128)S(1)}, s32[2048]{0:T(1024)S(1)}, s32[4,128]{1,0:T(4,128)S(1)}, s32[]{:T(128)}, ...), branch_computations={%region_10.10_spmd, %region_11.13_spmd} | conditional | flops 549324288 | bytes 26912820 | solution.py:108
  195.8 0.3 compare_and_fusion
  196.1 1.0 select_reduce_fusion
  197.1 1.2 fusion.18
  198.3 1.2 fusion.31
  199.6 0.7 constant_dynamic-update-slice_fusion.5
  200.4 1.3 divide_convert_fusion
  201.7 25.9 %while.34 = (s32[]{:T(128)}, bf16[4,128,4096]{2,1,0:T(8,128)(2,1)}, bf16[4,128,512]{1,2,0:T(8,128)(2,1)S(1)}, s32[4]{0:T(128)S(1)}, bf16[3,512,4096]{2,1,0:T(8,128)(2,1)}, /*index=5*/s32[]{:T(128)}, s32[]{:T(128)}, s32[]{:T(128)}) while((s32[]{:T(128)}, bf16[4,128,4096]{2,1,0:T(8,128)(2,1)}, bf16[4,128,512]{1,2,0:T(8,128)(2,1)S(1)}, ...), condition=%wide.region_16.17_spmd, body=%wide.region_15.16_spmd.sunk | while | flops 536870912 | bytes 6423687 | solution.py:122
  201.7 0.6 dynamic_slice.98
  204.3 3.9 %fusion.68 = bf16[4,128,4096]{2,1,0:T(8,128)(2,1)} fusion(bf16[4,128,4096]{2,1,0:T(8,128)(2,1)} %get-tuple-element.517, s32[]{:T(128)} %get-tuple-element.516, bf16[3,512,4096]{2,1,0:T(8,128)(2,1)} %get-tuple-element.528, s32[]{:T(128)S(6)} %select_n.68, bf16[4,128,512]{1,2,0:T(8,128)(2,1)S(1)} %get-tuple-element.526), kind=kOutput, calls=%fused_computation.36.clone.1 | convolution fusion | flops 536870912 | bytes 6423556 | tf_op jit(solution)/shard_map/while/body/eval_jaxpr/dot_general | solution.py:120
  208.2 0.6 dynamic_slice.98
  210.7 4.0 %fusion.68 = bf16[4,128,4096]{2,1,0:T(8,128)(2,1)} fusion(bf16[4,128,4096]{2,1,0:T(8,128)(2,1)} %get-tuple-element.517, s32[]{:T(128)} %get-tuple-element.516, bf16[3,512,4096]{2,1,0:T(8,128)(2,1)} %get-tuple-element.528, s32[]{:T(128)S(6)} %select_n.68, bf16[4,128,512]{1,2,0:T(8,128)(2,1)S(1)} %get-tuple-element.526), kind=kOutput, calls=%fused_computation.36.clone.1 | convolution fusion | flops 536870912 | bytes 6423556 | tf_op jit(solution)/shard_map/while/body/eval_jaxpr/dot_general | solution.py:120
  214.7 0.6 dynamic_slice.98
  217.3 3.9 %fusion.68 = bf16[4,128,4096]{2,1,0:T(8,128)(2,1)} fusion(bf16[4,128,4096]{2,1,0:T(8,128)(2,1)} %get-tuple-element.517, s32[]{:T(128)} %get-tuple-element.516, bf16[3,512,4096]{2,1,0:T(8,128)(2,1)} %get-tuple-element.528, s32[]{:T(128)S(6)} %select_n.68, bf16[4,128,512]{1,2,0:T(8,128)(2,1)S(1)} %get-tuple-element.526), kind=kOutput, calls=%fused_computation.36.clone.1 | convolution fusion | flops 536870912 | bytes 6423556 | tf_op jit(solution)/shard_map/while/body/eval_jaxpr/dot_general | solution.py:120
  221.2 0.6 dynamic_slice.98
  223.7 3.9 %fusion.68 = bf16[4,128,4096]{2,1,0:T(8,128)(2,1)} fusion(bf16[4,128,4096]{2,1,0:T(8,128)(2,1)} %get-tuple-element.517, s32[]{:T(128)} %get-tuple-element.516, bf16[3,512,4096]{2,1,0:T(8,128)(2,1)} %get-tuple-element.528, s32[]{:T(128)S(6)} %select_n.68, bf16[4,128,512]{1,2,0:T(8,128)(2,1)S(1)} %get-tuple-element.526), kind=kOutput, calls=%fused_computation.36.clone.1 | convolution fusion | flops 536870912 | bytes 6423556 | tf_op jit(solution)/shard_map/while/body/eval_jaxpr/dot_general | solution.py:120
  227.7 50.1 %reduce-scatter.2.cloned.1.call-done = bf16[64,4096]{1,0:T(8,128)(2,1)} async-done(((bf16[512,4096]{1,0:T(8,128)(2,1)}), bf16[64,4096]{1,0:T(8,128)(2,1)}) %reduce-scatter.2.cloned.1.call-update) | async-done | bytes 524304 | tf_op jit(solution)/shard_map/reduce_scatter | solution.py:125
  277.8 2.0 fusion.51
  (75 shorter events, 1.6 us)
Async XLA Ops:
  6.5 5.5 %copy-start.2 = (s32[16]{0:T(128)S(1)}, s32[16]{0:T(128)}, u32[]{:S(2)}) copy-start(s32[16]{0:T(128)} %param.18) | copy-start | bytes 196
  6.5 55.2 %all-gather.6.cloned.1.call-start = ((), (), s32[]{:S(2)}) async-start(), calls=%async_computation.1 | async-start | bytes 4718592 | tf_op jit(solution)/shard_map/all_gather | solution.py:38
  12.0 123.8 %all-gather.8.cloned.1.call-start = ((), (), s32[]{:S(2)}) async-start(), calls=%async_computation.3 | async-start | bytes 2621440 | tf_op jit(solution)/shard_map/all_gather | solution.py:72
  99.9 2.6 copy-start.3
  101.7 70.9 %all-gather.10.cloned.1.call-start = ((), (), s32[]{:S(2)}) async-start(), calls=%async_computation.4 | async-start | bytes 2621440 | tf_op jit(solution)/shard_map/all_gather | solution.py:73
  102.5 175.3 %reduce-scatter.2.cloned.1.call-start = ((), (), s32[]{:S(2)}) async-start(), calls=%async_computation.2 | async-start | bytes 4718592 | tf_op jit(solution)/shard_map/reduce_scatter | solution.py:125
  178.3 2.2 copy-start.1
  184.2 2.2 copy-start.1
  190.2 2.2 copy-start.1
  196.1 2.2 copy-start.1
  227.6 50.1 %copy-start = (bf16[64,4096]{1,0:T(8,128)(2,1)S(1)}, bf16[64,4096]{1,0:T(8,128)(2,1)}, u32[]{:S(2)}) copy-start(bf16[64,4096]{1,0:T(8,128)(2,1)} %param.14) | copy-start | bytes 1572868
Sparse Core Ops, SparseCore 0:
  12.1 49.5 all-gather.5
  101.9 33.8 all-gather.7
  137.6 35.0 all-gather.9
  227.8 49.9 reduce-scatter.1
where the time goes:
time: 287 us; the launch traced here: 286 us
  waiting for transfers between devices  167 us (58%)
  matrix products  51.3 us (18%)
  local copies, waits for them, and re-layouts  18.7 us (7%)
  loops' own time  18.6 us (6%)
  other arithmetic  17.4 us (6%)
  between operations  13.3 us (5%)
    reduce_scatter x1, waiting for transfers between devices, body(): lax.psum_scatter(partial_value.reshape(group_rows, partial_value.shape[2]...  50.1 us
    all_gather x1, waiting for transfers between devices, body(): gathered = lax.all_gather(normed, 'seq', axis=0, tiled=True)  49.6 us
    all_gather x1, waiting for transfers between devices, body(): piece_values = lax.all_gather(values_here, 'mod', axis=0, tiled=True)  33.9 us
    all_gather x1, waiting for transfers between devices, body(): piece_keys = lax.all_gather(keys_here, 'mod', axis=0, tiled=True)  32.5 us
    dot_general x4, matrix products, project(): jnp.dot(row_block, weight, preferred_element_type=jnp.float32)  26.9 us
    dot_general x4, matrix products, output(): return jnp.dot(row_block, weight, preferred_element_type=jnp.float32)  15.8 us
    another operation x1, loops' own time, body(): lax.map(project, (gathered.reshape(block_count, BLOCK, gathered.shape[1])...  7.85 us
    another operation x1, loops' own time, body(): lax.map(output, (attended.reshape(block_count, BLOCK, attended.shape[1]),...  7.79 us
  transfers between devices with their start and end apart: 4, of which 4 were waited for; matrix products, arithmetic and copies ran while one was open for 1% of the time, Pallas kernels for 0%

commit v1 on v0

--- a/solution.py
+++ b/solution.py
@@ -69,8 +69,18 @@
         jnp.zeros((block_total, block_size, heads_here, HDIM), jnp.float32),
     )
     key_start = jnp.int32(0)
-    piece_keys = lax.all_gather(keys_here, "mod", axis=0, tiled=True)
-    piece_values = lax.all_gather(values_here, "mod", axis=0, tiled=True)
+
+    def define_the_state(x0, frame_in):
+        last = jnp.split(
+            jax.lax.all_gather(
+                jnp.concatenate([x0, frame_in], axis=1), axis_name="mod", axis=0, tiled=True
+            ),
+            [x0.shape[1]],
+            axis=1,
+        )
+        return last
+
+    piece_keys, piece_values = define_the_state(keys_here, values_here)
     key_count = piece_keys.shape[0]
     key_pos = jnp.arange(key_count, dtype=jnp.int32)
     key_docs = documents(key_pos, doc_lengths)

time: 287 us -> 275 us (0.958)
  waiting for transfers between devices: 167 us -> 150 us
  local copies, waits for them, and re-layouts: 18.7 us -> 22.5 us
    all_gather x2 -> x1, waiting for transfers between devices: 66.4 us -> 50.6 us  [define_the_state(): jax.lax.all_gather(jnp.concatenate([x0, frame_in], axis=1), axis_name='mo...]
    split x0 -> x1, local copies, waits for them, and re-layouts: none -> 4.78 us  [define_the_state(): jnp.split(jax.lax.all_gather(jnp.concatenate([x0, frame_in], axis=1), axi...]
  transfers between devices with their start and end apart: 4 -> 3, of which waited for: 4 -> 3; matrix products, arithmetic and copies ran while one was open for 1% -> 0% of each run, Pallas kernels for 0% -> 0%
where the time goes in v1:
time: 275 us; the launch traced here: 274 us
  waiting for transfers between devices  150 us (55%)
  matrix products  51.3 us (19%)
  local copies, waits for them, and re-layouts  22.5 us (8%)
  other arithmetic  18.6 us (7%)
  loops' own time  18 us (7%)
  between operations  13.3 us (5%)
    all_gather x1, waiting for transfers between devices, define_the_state(): jax.lax.all_gather(jnp.concatenate([x0, frame_in], axis=1), axis_name='mo...  50.6 us
    reduce_scatter x1, waiting for transfers between devices, body(): lax.psum_scatter(partial_value.reshape(group_rows, partial_value.shape[2]...  50.1 us
    all_gather x1, waiting for transfers between devices, body(): gathered = lax.all_gather(normed, 'seq', axis=0, tiled=True)  49.6 us
    dot_general x4, matrix products, project(): jnp.dot(row_block, weight, preferred_element_type=jnp.float32)  26.9 us
    dot_general x4, matrix products, output(): return jnp.dot(row_block, weight, preferred_element_type=jnp.float32)  15.8 us
    another operation x1, loops' own time, body(): lax.map(project, (gathered.reshape(block_count, BLOCK, gathered.shape[1])...  7.85 us
    another operation x1, loops' own time, body(): lax.map(output, (attended.reshape(block_count, BLOCK, attended.shape[1]),...  7.44 us
    unnamed x9, local copies, waits for them, and re-layouts  7.06 us
  transfers between devices with their start and end apart: 3, of which 3 were waited for; matrix products, arithmetic and copies ran while one was open for 0% of the time, Pallas kernels for 0%

profile of v1, /device:TPU:0, one launch (start us, length us, event | category | flops | bytes accessed | tf_op | source)
XLA Modules:
  0.0 274.1 jit_solution(4672608113789526536)
XLA Ops:
  6.6 0.8 select_reduce_fusion.2
  7.4 1.2 fusion.48
  8.6 1.3 select_reduce_fusion.1
  9.9 2.0 fusion.50
  12.2 49.6 %all-gather.3.cloned.1.call-done = bf16[512,4096]{1,0:T(8,128)(2,1)} async-done(((bf16[64,4096]{1,0:T(8,128)(2,1)}), bf16[512,4096]{1,0:T(8,128)(2,1)}) %all-gather.3.cloned.1.call-update) | async-done | bytes 4194320 | tf_op jit(solution)/shard_map/all_gather | solution.py:38
  61.7 37.1 %while.33 = (s32[]{:T(128)}, bf16[4,128,1536]{2,1,0:T(8,128)(2,1)S(1)}, bf16[4,128,4096]{2,1,0:T(8,128)(2,1)}, s32[4]{0:T(128)S(1)}, bf16[3,4096,1536]{2,1,0:T(8,128)(2,1)}, /*index=5*/s32[]{:T(128)}, s32[]{:T(128)}, s32[]{:T(128)}) while((s32[]{:T(128)}, bf16[4,128,1536]{2,1,0:T(8,128)(2,1)S(1)}, bf16[4,128,4096]{2,1,0:T(8,128)(2,1)}, ...), condition=%wide.region_4.5_spmd, body=%wide.region_3.4_spmd.sunk | while | flops 1610809344 | bytes 14025863 | solution.py:49
  61.7 0.6 dynamic_slice.95
  64.3 6.7 %fusion.65 = bf16[4,128,1536]{2,1,0:T(8,128)(2,1)S(1)} fusion(bf16[4,128,1536]{2,1,0:T(8,128)(2,1)S(1)} %get-tuple-element.459, s32[]{:T(128)} %get-tuple-element.458, bf16[3,4096,1536]{2,1,0:T(8,128)(2,1)} %get-tuple-element.470, s32[]{:T(128)S(6)} %select_n.67, bf16[4,128,4096]{2,1,0:T(8,128)(2,1)} %get-tuple-element.468), kind=kOutput, calls=%fused_computation.6.clone.1 | convolution fusion | flops 1610809344 | bytes 14025732 | tf_op jit(solution)/shard_map/while/body/eval_jaxpr/dot_general | solution.py:47
  71.0 0.6 dynamic_slice.95
  73.5 6.7 %fusion.65 = bf16[4,128,1536]{2,1,0:T(8,128)(2,1)S(1)} fusion(bf16[4,128,1536]{2,1,0:T(8,128)(2,1)S(1)} %get-tuple-element.459, s32[]{:T(128)} %get-tuple-element.458, bf16[3,4096,1536]{2,1,0:T(8,128)(2,1)} %get-tuple-element.470, s32[]{:T(128)S(6)} %select_n.67, bf16[4,128,4096]{2,1,0:T(8,128)(2,1)} %get-tuple-element.468), kind=kOutput, calls=%fused_computation.6.clone.1 | convolution fusion | flops 1610809344 | bytes 14025732 | tf_op jit(solution)/shard_map/while/body/eval_jaxpr/dot_general | solution.py:47
  80.3 0.6 dynamic_slice.95
  82.8 6.7 %fusion.65 = bf16[4,128,1536]{2,1,0:T(8,128)(2,1)S(1)} fusion(bf16[4,128,1536]{2,1,0:T(8,128)(2,1)S(1)} %get-tuple-element.459, s32[]{:T(128)} %get-tuple-element.458, bf16[3,4096,1536]{2,1,0:T(8,128)(2,1)} %get-tuple-element.470, s32[]{:T(128)S(6)} %select_n.67, bf16[4,128,4096]{2,1,0:T(8,128)(2,1)} %get-tuple-element.468), kind=kOutput, calls=%fused_computation.6.clone.1 | convolution fusion | flops 1610809344 | bytes 14025732 | tf_op jit(solution)/shard_map/while/body/eval_jaxpr/dot_general | solution.py:47
  89.5 0.6 dynamic_slice.95
  92.1 6.7 %fusion.65 = bf16[4,128,1536]{2,1,0:T(8,128)(2,1)S(1)} fusion(bf16[4,128,1536]{2,1,0:T(8,128)(2,1)S(1)} %get-tuple-element.459, s32[]{:T(128)} %get-tuple-element.458, bf16[3,4096,1536]{2,1,0:T(8,128)(2,1)} %get-tuple-element.470, s32[]{:T(128)S(6)} %select_n.67, bf16[4,128,4096]{2,1,0:T(8,128)(2,1)} %get-tuple-element.468), kind=kOutput, calls=%fused_computation.6.clone.1 | convolution fusion | flops 1610809344 | bytes 14025732 | tf_op jit(solution)/shard_map/while/body/eval_jaxpr/dot_general | solution.py:47
  98.8 1.1 copy.15
  99.9 0.6 reshape.161
  100.7 1.2 pad_maximum_fusion
  102.0 0.2 reduce-window.8
  102.4 0.3 copy.16
  102.7 50.6 %all-gather.5.cloned.1.call-done = bf16[2048,8,128]{0,2,1:T(8,128)(2,1)} async-done(((bf16[512,8,128]{0,2,1:T(8,128)(2,1)}), bf16[2048,8,128]{0,2,1:T(8,128)(2,1)}) %all-gather.5.cloned.1.call-update) | async-done | bytes 4194320 | tf_op jit(solution)/shard_map/all_gather | solution.py:75
  153.3 4.8 %fusion.53 = (bf16[2048,4,128]{0,2,1:T(8,128)(2,1)}, bf16[2048,4,128]{0,2,1:T(8,128)(2,1)}) fusion(bf16[2048,8,128]{0,2,1:T(8,128)(2,1)} %all-gather.5.cloned.1.call-done), kind=kLoop, calls=%fused_computation.71 | loop fusion | bytes 8388608 | tf_op jit(solution)/shard_map/split | solution.py:74
  158.1 3.0 %copy.19 = bf16[2048,4,128]{2,0,1:T(8,128)(2,1)S(1)} copy(bf16[2048,4,128]{0,2,1:T(8,128)(2,1)} %get-tuple-element.317) | data formatting | bytes 4194304
  161.1 4.0 %copy.20 = bf16[2048,4,128]{2,0,1:T(8,128)(2,1)} copy(bf16[2048,4,128]{0,2,1:T(8,128)(2,1)} %get-tuple-element.316) | data formatting | bytes 4194304
  165.1 23.5 %while.35 = (s32[]{:T(128)}, f32[4,4,128]{2,1,0:T(4,128)S(1)}, f32[4,128,4,128]{1,3,2,0:T(8,128)}, s32[4,128]{1,0:T(4,128)S(1)}, s32[2048]{0:T(1024)S(1)}, /*ind...) while((s32[]{:T(128)}, f32[4,4,128]{2,1,0:T(4,128)S(1)}, ...), condition=%wide.region_14.15_spmd.clone, body=%wide.region_8.14_spmd.clone.sunk | while | flops 549324416 | bytes 28503860 | solution.py:120
  165.1 0.6 fusion.69
  166.4 3.7 %conditional.3 = (f32[1,4,128]{2,1,0:T(4,128)S(1)}, f32[1,128,4,128]{3,1,2,0:T(8,128)S(1)}) conditional(s32[]{:T(128)} %convert_element_type.82, (f32[4,128]{1,0:T(4,128)S(1)}, f32[128,4,128]{2,0,1:T(8,128)S(1)}) %tuple.106, (s32[2048]{0:T(1024)S(1)}, s32[1,128]{1,0:T(1,128)S(1)}, s32[2048]{0:T(1024)S(1)}, s32[4,128]{1,0:T(4,128)S(1)}, s32[]{:T(128)}, ...), branch_computations={%region_10.10_spmd, %region_11.13_spmd} | conditional | flops 549324288 | bytes 26912820 | solution.py:118
  166.4 0.3 compare_and_fusion
  166.7 1.0 select_reduce_fusion
  167.7 1.2 fusion.18
  168.9 1.2 fusion.31
  170.2 0.7 constant_dynamic-update-slice_fusion.5
  170.9 0.6 fusion.69
  172.2 3.7 %conditional.3 = (f32[1,4,128]{2,1,0:T(4,128)S(1)}, f32[1,128,4,128]{3,1,2,0:T(8,128)S(1)}) conditional(s32[]{:T(128)} %convert_element_type.82, (f32[4,128]{1,0:T(4,128)S(1)}, f32[128,4,128]{2,0,1:T(8,128)S(1)}) %tuple.106, (s32[2048]{0:T(1024)S(1)}, s32[1,128]{1,0:T(1,128)S(1)}, s32[2048]{0:T(1024)S(1)}, s32[4,128]{1,0:T(4,128)S(1)}, s32[]{:T(128)}, ...), branch_computations={%region_10.10_spmd, %region_11.13_spmd} | conditional | flops 549324288 | bytes 26912820 | solution.py:118
  172.3 0.3 compare_and_fusion
  172.6 1.0 select_reduce_fusion
  173.6 1.2 fusion.18
  174.7 1.2 fusion.31
  176.1 0.7 constant_dynamic-update-slice_fusion.5
  176.8 0.6 fusion.69
  178.1 3.7 %conditional.3 = (f32[1,4,128]{2,1,0:T(4,128)S(1)}, f32[1,128,4,128]{3,1,2,0:T(8,128)S(1)}) conditional(s32[]{:T(128)} %convert_element_type.82, (f32[4,128]{1,0:T(4,128)S(1)}, f32[128,4,128]{2,0,1:T(8,128)S(1)}) %tuple.106, (s32[2048]{0:T(1024)S(1)}, s32[1,128]{1,0:T(1,128)S(1)}, s32[2048]{0:T(1024)S(1)}, s32[4,128]{1,0:T(4,128)S(1)}, s32[]{:T(128)}, ...), branch_computations={%region_10.10_spmd, %region_11.13_spmd} | conditional | flops 549324288 | bytes 26912820 | solution.py:118
  178.1 0.3 compare_and_fusion
  178.4 1.0 select_reduce_fusion
  179.4 1.2 fusion.18
  180.6 1.2 fusion.31
  181.9 0.7 constant_dynamic-update-slice_fusion.5
  182.7 0.6 fusion.69
  184.0 3.7 %conditional.3 = (f32[1,4,128]{2,1,0:T(4,128)S(1)}, f32[1,128,4,128]{3,1,2,0:T(8,128)S(1)}) conditional(s32[]{:T(128)} %convert_element_type.82, (f32[4,128]{1,0:T(4,128)S(1)}, f32[128,4,128]{2,0,1:T(8,128)S(1)}) %tuple.106, (s32[2048]{0:T(1024)S(1)}, s32[1,128]{1,0:T(1,128)S(1)}, s32[2048]{0:T(1024)S(1)}, s32[4,128]{1,0:T(4,128)S(1)}, s32[]{:T(128)}, ...), branch_computations={%region_10.10_spmd, %region_11.13_spmd} | conditional | flops 549324288 | bytes 26912820 | solution.py:118
  184.0 0.3 compare_and_fusion
  184.3 1.0 select_reduce_fusion
  185.3 1.2 fusion.18
  186.5 1.2 fusion.31
  187.8 0.7 constant_dynamic-update-slice_fusion.5
  188.6 1.3 divide_convert_fusion
  189.9 25.6 %while.34 = (s32[]{:T(128)}, bf16[4,128,4096]{2,1,0:T(8,128)(2,1)}, bf16[4,128,512]{1,2,0:T(8,128)(2,1)S(1)}, s32[4]{0:T(128)S(1)}, bf16[3,512,4096]{2,1,0:T(8,128)(2,1)}, /*index=5*/s32[]{:T(128)}, s32[]{:T(128)}, s32[]{:T(128)}) while((s32[]{:T(128)}, bf16[4,128,4096]{2,1,0:T(8,128)(2,1)}, bf16[4,128,512]{1,2,0:T(8,128)(2,1)S(1)}, ...), condition=%wide.region_16.17_spmd, body=%wide.region_15.16_spmd.sunk | while | flops 536870912 | bytes 6423687 | solution.py:132
  189.9 0.6 dynamic_slice.98
  192.4 3.9 %fusion.68 = bf16[4,128,4096]{2,1,0:T(8,128)(2,1)} fusion(bf16[4,128,4096]{2,1,0:T(8,128)(2,1)} %get-tuple-element.519, s32[]{:T(128)} %get-tuple-element.518, bf16[3,512,4096]{2,1,0:T(8,128)(2,1)} %get-tuple-element.530, s32[]{:T(128)S(6)} %select_n.68, bf16[4,128,512]{1,2,0:T(8,128)(2,1)S(1)} %get-tuple-element.528), kind=kOutput, calls=%fused_computation.36.clone.1 | convolution fusion | flops 536870912 | bytes 6423556 | tf_op jit(solution)/shard_map/while/body/eval_jaxpr/dot_general | solution.py:130
  196.3 0.6 dynamic_slice.98
  198.8 4.0 %fusion.68 = bf16[4,128,4096]{2,1,0:T(8,128)(2,1)} fusion(bf16[4,128,4096]{2,1,0:T(8,128)(2,1)} %get-tuple-element.519, s32[]{:T(128)} %get-tuple-element.518, bf16[3,512,4096]{2,1,0:T(8,128)(2,1)} %get-tuple-element.530, s32[]{:T(128)S(6)} %select_n.68, bf16[4,128,512]{1,2,0:T(8,128)(2,1)S(1)} %get-tuple-element.528), kind=kOutput, calls=%fused_computation.36.clone.1 | convolution fusion | flops 536870912 | bytes 6423556 | tf_op jit(solution)/shard_map/while/body/eval_jaxpr/dot_general | solution.py:130
  202.7 0.6 dynamic_slice.98
  205.2 3.9 %fusion.68 = bf16[4,128,4096]{2,1,0:T(8,128)(2,1)} fusion(bf16[4,128,4096]{2,1,0:T(8,128)(2,1)} %get-tuple-element.519, s32[]{:T(128)} %get-tuple-element.518, bf16[3,512,4096]{2,1,0:T(8,128)(2,1)} %get-tuple-element.530, s32[]{:T(128)S(6)} %select_n.68, bf16[4,128,512]{1,2,0:T(8,128)(2,1)S(1)} %get-tuple-element.528), kind=kOutput, calls=%fused_computation.36.clone.1 | convolution fusion | flops 536870912 | bytes 6423556 | tf_op jit(solution)/shard_map/while/body/eval_jaxpr/dot_general | solution.py:130
  209.1 0.6 dynamic_slice.98
  211.6 3.9 %fusion.68 = bf16[4,128,4096]{2,1,0:T(8,128)(2,1)} fusion(bf16[4,128,4096]{2,1,0:T(8,128)(2,1)} %get-tuple-element.519, s32[]{:T(128)} %get-tuple-element.518, bf16[3,512,4096]{2,1,0:T(8,128)(2,1)} %get-tuple-element.530, s32[]{:T(128)S(6)} %select_n.68, bf16[4,128,512]{1,2,0:T(8,128)(2,1)S(1)} %get-tuple-element.528), kind=kOutput, calls=%fused_computation.36.clone.1 | convolution fusion | flops 536870912 | bytes 6423556 | tf_op jit(solution)/shard_map/while/body/eval_jaxpr/dot_general | solution.py:130
  215.5 50.1 %reduce-scatter.2.cloned.1.call-done = bf16[64,4096]{1,0:T(8,128)(2,1)} async-done(((bf16[512,4096]{1,0:T(8,128)(2,1)}), bf16[64,4096]{1,0:T(8,128)(2,1)}) %reduce-scatter.2.cloned.1.call-update) | async-done | bytes 524304 | tf_op jit(solution)/shard_map/reduce_scatter | solution.py:135
  265.6 2.0 fusion.51
  (74 shorter events, 1.4 us)
Async XLA Ops:
  6.5 5.5 %copy-start.2 = (s32[16]{0:T(128)S(1)}, s32[16]{0:T(128)}, u32[]{:S(2)}) copy-start(s32[16]{0:T(128)} %param.18) | copy-start | bytes 196
  6.5 55.2 %all-gather.3.cloned.1.call-start = ((), (), s32[]{:S(2)}) async-start(), calls=%async_computation.1 | async-start | bytes 4718592 | tf_op jit(solution)/shard_map/all_gather | solution.py:38
  12.0 141.3 %all-gather.5.cloned.1.call-start = ((), (), s32[]{:S(2)}) async-start(), calls=%async_computation.2 | async-start | bytes 5242880 | tf_op jit(solution)/shard_map/all_gather | solution.py:75
  99.9 2.0 copy-start.3
  101.9 163.7 %reduce-scatter.2.cloned.1.call-start = ((), (), s32[]{:S(2)}) async-start(), calls=%async_computation.3 | async-start | bytes 4718592 | tf_op jit(solution)/shard_map/reduce_scatter | solution.py:135
  166.7 2.2 copy-start.1
  172.6 2.2 copy-start.1
  178.4 2.2 copy-start.1
  184.3 2.2 copy-start.1
  215.5 50.1 %copy-start = (bf16[64,4096]{1,0:T(8,128)(2,1)S(1)}, bf16[64,4096]{1,0:T(8,128)(2,1)}, u32[]{:S(2)}) copy-start(bf16[64,4096]{1,0:T(8,128)(2,1)} %param.14) | copy-start | bytes 1572868
Sparse Core Ops, SparseCore 0:
  12.1 49.5 all-gather.2
  102.0 51.2 all-gather.4
  215.6 49.9 reduce-scatter.1
